TPU v7x, 256 devices: a whole 4x4x8 slice. The times are simulated.
256 devices in a mesh: row: 8 (over y, core), col: 32 (over z, x).
Axes of the slice: x: 4, y: 4, z: 8, core: 2. Of those that a mesh axis runs over, the one named last changes fastest.
Arguments:
- queries: bfloat16 [1024, 128, 1024], P(('row', 'col')), may hold values from -6 to 6
- coarse_keys: bfloat16 [2048, 1024], P('row'), may hold values from -6 to 6
- fine_keys: bfloat16 [16384, 1024], P('col'), may hold values from -6 to 6
- super_ids: int32 [1024, 16], P(('row', 'col')), may hold values from 0 to 2047, as said below
- picks: int32 [1024, 64], P(('row', 'col')), may hold values from 0 to 127, as said below
Outputs:
- importance: float32 [1024, 8, 2048], P(('row', 'col'))
- selected: float32 [1024, 512], P(('row', 'col'))
Inputs may be any that keep to these rules, and one draw needn't show every extreme that they name: `super_ids`: within each aligned run of 4 query blocks (the query blocks of one device), at most 16 of the ids lie in any one aligned range of 64 superblocks, and some range holds exactly 16; in some aligned group of 32 consecutive runs, one range holds exactly 16 ids of every run. Ids may repeat. `picks`: the numbers of a row are distinct; pick p names fine block p % 8 of superblock super_ids[b, p // 8]. Within each aligned run of 4 query blocks, at most 64 of the named fine blocks lie in any one aligned range of 64 superblocks, and some range holds exactly 64.
All inputs are finite; a program needn't handle non-finite values.
Results may differ from a plain program's by a relative error of at most 0.0003.
Values may be sent and summed in bfloat16 or wider, within the bound.
A program may use at most 64 MiB of HBM per device.

v0:
```python
import math

import jax
import jax.numpy as jnp
from jax import lax
from jax.sharding import PartitionSpec as P

H = 8
D = 128
SBLK = 8
PICK = 64


def pack_requests(owners, local_ids, ncols, capacity):
    marks = (owners[:, None] == jnp.arange(ncols, dtype=jnp.int32)[None, :]).astype(jnp.int32)
    earlier = jnp.cumsum(marks, axis=0) - marks
    slots = jnp.sum(earlier * marks, axis=1)
    places = owners * capacity + slots
    cells = jnp.arange(ncols * capacity, dtype=jnp.int32)
    matches = places[:, None] == cells[None, :]
    outgoing = jnp.sum(jnp.where(matches, local_ids[:, None] + 1, 0), axis=0) - 1
    return (outgoing.reshape(ncols, capacity), places)


def per_device(queries, coarse_keys, fine_keys, super_ids, picks):
    factor = 1.0 / math.sqrt(D)
    blocks, qtok, width = queries.shape
    supers = coarse_keys.shape[0] * lax.axis_size("row")
    ncols = lax.axis_size("col")
    qheads = queries.reshape(blocks, qtok, H, D)

    def block_scores(query_block, block_keys):
        keyed = block_keys.reshape(block_keys.shape[0], H, D)
        return (
            jnp.einsum("thd,nhd->htn", query_block, keyed, preferred_element_type=jnp.float32)
            * factor
        )

    start_max = jnp.full((blocks, H, qtok), -1e30, jnp.float32)
    start_totals = jnp.zeros((blocks, H, qtok), jnp.float32)
    gathered = lax.all_gather(coarse_keys, "row", axis=0, tiled=True)

    def stat_per_block(inputs):
        query_block, running_max, totals = inputs
        scores = block_scores(query_block, gathered)
        new_max = jnp.maximum(running_max, jnp.max(scores, axis=-1))
        totals = totals * jnp.exp(running_max - new_max) + jnp.sum(
            jnp.exp(scores - new_max[..., None]), axis=-1
        )
        return (new_max, totals)

    running_max, totals = lax.map(stat_per_block, (qheads, start_max, start_totals))

    def make_per_block(inputs):
        query_block, block_max, block_totals = inputs
        scores = block_scores(query_block, gathered)
        softened = jnp.exp(scores - block_max[..., None]) / block_totals[..., None]
        return jnp.sum(softened, axis=1) * (supers / qtok)

    portion = lax.map(make_per_block, (qheads, running_max, totals))
    sup_dev = fine_keys.shape[0] // SBLK
    parents = jnp.take_along_axis(super_ids, picks // SBLK, axis=1)
    capacity = blocks // 4 * PICK
    span = sup_dev * SBLK
    fine_ids = parents * SBLK + picks % SBLK
    owners = (fine_ids // span).reshape(-1)
    local_ids = (fine_ids % span).reshape(-1)
    outgoing, places = pack_requests(owners, local_ids, ncols, capacity)
    found = jnp.take(
        fine_keys,
        jnp.clip(
            lax.all_to_all(outgoing, "col", split_axis=0, concat_axis=0, tiled=True), 0, span - 1
        ),
        axis=0,
    )
    replies = lax.all_to_all(found, "col", split_axis=0, concat_axis=0, tiled=True)
    fetched = jnp.take(replies.reshape(ncols * capacity, width), places, axis=0)
    fetched = fetched.reshape(blocks, PICK, H, D)
    weights = jnp.take_along_axis(
        portion, jnp.broadcast_to(parents[:, None, :], (blocks, H, PICK)), axis=2
    )
    scores = (
        jnp.einsum("bthd,bjhd->bhtj", qheads, fetched, preferred_element_type=jnp.float32) * factor
    )
    softened = jax.nn.softmax(scores, axis=-1)
    selected = jnp.sum(softened, axis=2) * weights * (PICK / qtok)
    return (portion, selected.reshape(blocks, H * PICK))


def solution(mesh):
    return jax.shard_map(
        per_device,
        mesh=mesh,
        in_specs=(
            P(("row", "col"), None, None),
            P("row", None),
            P("col", None),
            P(("row", "col"), None),
            P(("row", "col"), None),
        ),
        out_specs=(P(("row", "col"), None, None), P(("row", "col"), None)),
        check_vma=False,
    )
```

profile of v0, /device:TPU:7, one launch (start us, length us, event | category | flops | bytes accessed | tf_op | source)
XLA Modules:
  0.0 161.8 jit_solution(1357026586187188724)
XLA Ops:
  8.7 2.3 %gather_fusion.2 = s32[256]{0:T(256)S(1)} fusion(s32[4,16]{1,0:T(4,128)} %param.12, s32[256]{0:T(256)S(1)} %reshape.247), kind=kCustom, calls=%fused_computation.2 | custom fusion | bytes 4096 | tf_op jit(solution)/shard_map/jit(take_along_axis)/gather | solution.py:62
  14.7 11.0 %all-to-all-start = ((s32[32,1,64]{2,1,0:T(1,128)}), s32[32,1,64]{2,1,0:T(1,128)S(1)}, u32[]{:S(2)}, u32[]{:S(2)}) async-start(s32[32,1,64]{2,1,0:T(1,128)} %sub.59), calls=%async_computation | async-start | bytes 32768 | tf_op jit(solution)/shard_map/all_to_all | solution.py:72
  26.0 1.7 %copy.28 = bf16[4,128,1024]{1,2,0:T(8,128)(2,1)S(1)} copy(bf16[4,128,1024]{2,1,0:T(8,128)(2,1)} %param.9) | data formatting | bytes 2097152 | tf_op args[0]
  28.4 4.3 %all-to-all-done = s32[32,1,64]{2,1,0:T(1,128)S(1)} async-done(((s32[32,1,64]{2,1,0:T(1,128)}), s32[32,1,64]{2,1,0:T(1,128)S(1)}, u32[]{:S(2)}, u32[]{:S(2)}) %all-to-all-start) | async-done | bytes 8224 | tf_op jit(solution)/shard_map/all_to_all | solution.py:72
  32.9 9.7 %gather_fusion = bf16[2048,1024]{1,0:T(8,128)(2,1)} fusion(bf16[512,1024]{1,0:T(8,128)(2,1)S(1)} %copy-done, s32[2048]{0:T(1024)S(1)} %broadcast_clamp_fusion.1), kind=kCustom, calls=%fused_computation | custom fusion | bytes 8396800 | tf_op jit(solution)/shard_map/jit(_take)/gather | solution.py:69
  42.6 3.9 %broadcast_select_fusion = bf16[32,64,1024]{2,1,0:T(8,128)(2,1)} fusion(bf16[32,64,1024]{2,1,0:T(8,128)(2,1)} %bitcast.109, pred[32,64]{1,0:T(8,128)(4,1)S(1)} %compare_and_fusion), kind=kLoop, calls=%fused_computation.31 | loop fusion | flops 2097152 | bytes 8390656 | tf_op jit(solution)/shard_map/jit(_take)/select_n | solution.py:69
  46.5 6.2 %all-to-all-start.1 = ((bf16[32,64,1024]{2,1,0:T(8,128)(2,1)}), bf16[32,64,1024]{2,1,0:T(8,128)(2,1)}, u32[]{:S(2)}, u32[]{:S(2)}) async-start(bf16[32,64,1024]{2,1,0:T(8,128)(2,1)} %broadcast_select_fusion), calls=%async_computation.1 | async-start | bytes 8388608 | tf_op jit(solution)/shard_map/all_to_all | solution.py:76
  52.7 21.0 %while.22 = (s32[]{:T(128)}, f32[4,8,128]{2,1,0:T(8,128)S(1)}, f32[4,8,128]{2,1,0:T(8,128)S(1)}, bf16[4,128,8,128]{3,1,2,0:T(8,128)(2,1)S(1)}, bf16[2048,1024]{1,0:T(8,128)(2,1)}, /*index=5*/s32[]{:T(128)}) while((s32[]{:T(128)}, f32[4,8,128]{2,1,0:T(8,128)S(1)}, f32[4,8,128]{2,1,0:T(8,128)S(1)}, bf16[4,128,8,128]{3,1,2,0:T(8,128)(2,1)S(1)}, ...), condition=%wide.region_3.4_spmd, body=%wide.region_0.3_spmd.sunk | while | flops 547359744 | bytes 21270604 | solution.py:52
  52.7 3.5 %multiply_reduce_fusion.2 = (f32[8,128]{1,0:T(8,128)S(1)}, f32[8,128,2048]{2,1,0:T(8,128)S(1)}) fusion(bf16[4,128,8,128]{3,1,2,0:T(8,128)(2,1)S(1)} %get-tuple-element.227, s32[]{:T(128)} %get-tuple-element.218, bf16[2048,1024]{1,0:T(8,128)(2,1)} %get-tuple-element.228), kind=kOutput, calls=%fused_computation.5.clone.1 | convolution fusion | flops 541064192 | bytes 12849156 | tf_op jit(solution)/shard_map/while/body/eval_jaxpr/thd,nhd->htn/dot_general | solution.py:35
  56.3 1.6 %exponential_reduce_fusion.2 = f32[8,128]{1,0:T(8,128)S(1)} fusion(f32[8,128,2048]{2,1,0:T(8,128)S(1)} %get-tuple-element.200, f32[8,128]{1,0:T(8,128)S(1)} %broadcast_maximum_fusion.2), kind=kLoop, calls=%fused_computation.4.clone.1 | loop fusion | flops 6290432 | bytes 8396800 | tf_op jit(solution)/shard_map/while/body/eval_jaxpr/reduce_sum | solution.py:47
  58.0 3.5 %multiply_reduce_fusion.2 = (f32[8,128]{1,0:T(8,128)S(1)}, f32[8,128,2048]{2,1,0:T(8,128)S(1)}) fusion(bf16[4,128,8,128]{3,1,2,0:T(8,128)(2,1)S(1)} %get-tuple-element.227, s32[]{:T(128)} %get-tuple-element.218, bf16[2048,1024]{1,0:T(8,128)(2,1)} %get-tuple-element.228), kind=kOutput, calls=%fused_computation.5.clone.1 | convolution fusion | flops 541064192 | bytes 12849156 | tf_op jit(solution)/shard_map/while/body/eval_jaxpr/thd,nhd->htn/dot_general | solution.py:35
  61.5 1.6 %exponential_reduce_fusion.2 = f32[8,128]{1,0:T(8,128)S(1)} fusion(f32[8,128,2048]{2,1,0:T(8,128)S(1)} %get-tuple-element.200, f32[8,128]{1,0:T(8,128)S(1)} %broadcast_maximum_fusion.2), kind=kLoop, calls=%fused_computation.4.clone.1 | loop fusion | flops 6290432 | bytes 8396800 | tf_op jit(solution)/shard_map/while/body/eval_jaxpr/reduce_sum | solution.py:47
  63.2 3.5 %multiply_reduce_fusion.2 = (f32[8,128]{1,0:T(8,128)S(1)}, f32[8,128,2048]{2,1,0:T(8,128)S(1)}) fusion(bf16[4,128,8,128]{3,1,2,0:T(8,128)(2,1)S(1)} %get-tuple-element.227, s32[]{:T(128)} %get-tuple-element.218, bf16[2048,1024]{1,0:T(8,128)(2,1)} %get-tuple-element.228), kind=kOutput, calls=%fused_computation.5.clone.1 | convolution fusion | flops 541064192 | bytes 12849156 | tf_op jit(solution)/shard_map/while/body/eval_jaxpr/thd,nhd->htn/dot_general | solution.py:35
  66.8 1.6 %exponential_reduce_fusion.2 = f32[8,128]{1,0:T(8,128)S(1)} fusion(f32[8,128,2048]{2,1,0:T(8,128)S(1)} %get-tuple-element.200, f32[8,128]{1,0:T(8,128)S(1)} %broadcast_maximum_fusion.2), kind=kLoop, calls=%fused_computation.4.clone.1 | loop fusion | flops 6290432 | bytes 8396800 | tf_op jit(solution)/shard_map/while/body/eval_jaxpr/reduce_sum | solution.py:47
  68.5 3.5 %multiply_reduce_fusion.2 = (f32[8,128]{1,0:T(8,128)S(1)}, f32[8,128,2048]{2,1,0:T(8,128)S(1)}) fusion(bf16[4,128,8,128]{3,1,2,0:T(8,128)(2,1)S(1)} %get-tuple-element.227, s32[]{:T(128)} %get-tuple-element.218, bf16[2048,1024]{1,0:T(8,128)(2,1)} %get-tuple-element.228), kind=kOutput, calls=%fused_computation.5.clone.1 | convolution fusion | flops 541064192 | bytes 12849156 | tf_op jit(solution)/shard_map/while/body/eval_jaxpr/thd,nhd->htn/dot_general | solution.py:35
  72.0 1.6 %exponential_reduce_fusion.2 = f32[8,128]{1,0:T(8,128)S(1)} fusion(f32[8,128,2048]{2,1,0:T(8,128)S(1)} %get-tuple-element.200, f32[8,128]{1,0:T(8,128)S(1)} %broadcast_maximum_fusion.2), kind=kLoop, calls=%fused_computation.4.clone.1 | loop fusion | flops 6290432 | bytes 8396800 | tf_op jit(solution)/shard_map/while/body/eval_jaxpr/reduce_sum | solution.py:47
  73.7 26.4 %while.23 = (s32[]{:T(128)}, f32[4,8,2048]{2,1,0:T(8,128)S(1)}, bf16[4,128,8,128]{3,1,2,0:T(8,128)(2,1)S(1)}, bf16[2048,1024]{1,0:T(8,128)(2,1)}, f32[4,8,128]{2...) while((s32[]{:T(128)}, f32[4,8,2048]{2,1,0:T(8,128)S(1)}, bf16[4,128,8,128]{3,1,2,0:T(8,128)(2,1)S(1)}, ...), condition=%wide.region_6.7_spmd, body=%wide.region_4.6_spmd.sunk | while | flops 545259520 | bytes 4677721 | solution.py:60
  73.7 6.5 %fusion.50 = f32[8,2048]{1,0:T(8,128)S(1)} fusion(f32[8,128]{1,0:T(8,128)S(1)} %get-tuple-element.210, f32[8,128]{1,0:T(8,128)S(1)} %get-tuple-element.211, bf16[4,128,8,128]{3,1,2,0:T(8,128)(2,1)S(1)} %get-tuple-element.246, s32[]{:T(128)} %get-tuple-element.237, bf16[2048,1024]{1,0:T(8,128)(2,1)} %get-tuple-element.247), kind=kOutput, calls=%fused_computation.20.clone.1 | convolution fusion | flops 545243136 | bytes 4530180 | tf_op jit(solution)/shard_map/while/body/eval_jaxpr/thd,nhd->htn/dot_general | solution.py:35
  80.3 6.5 %fusion.50 = f32[8,2048]{1,0:T(8,128)S(1)} fusion(f32[8,128]{1,0:T(8,128)S(1)} %get-tuple-element.210, f32[8,128]{1,0:T(8,128)S(1)} %get-tuple-element.211, bf16[4,128,8,128]{3,1,2,0:T(8,128)(2,1)S(1)} %get-tuple-element.246, s32[]{:T(128)} %get-tuple-element.237, bf16[2048,1024]{1,0:T(8,128)(2,1)} %get-tuple-element.247), kind=kOutput, calls=%fused_computation.20.clone.1 | convolution fusion | flops 545243136 | bytes 4530180 | tf_op jit(solution)/shard_map/while/body/eval_jaxpr/thd,nhd->htn/dot_general | solution.py:35
  86.9 6.5 %fusion.50 = f32[8,2048]{1,0:T(8,128)S(1)} fusion(f32[8,128]{1,0:T(8,128)S(1)} %get-tuple-element.210, f32[8,128]{1,0:T(8,128)S(1)} %get-tuple-element.211, bf16[4,128,8,128]{3,1,2,0:T(8,128)(2,1)S(1)} %get-tuple-element.246, s32[]{:T(128)} %get-tuple-element.237, bf16[2048,1024]{1,0:T(8,128)(2,1)} %get-tuple-element.247), kind=kOutput, calls=%fused_computation.20.clone.1 | convolution fusion | flops 545243136 | bytes 4530180 | tf_op jit(solution)/shard_map/while/body/eval_jaxpr/thd,nhd->htn/dot_general | solution.py:35
  93.5 6.5 %fusion.50 = f32[8,2048]{1,0:T(8,128)S(1)} fusion(f32[8,128]{1,0:T(8,128)S(1)} %get-tuple-element.210, f32[8,128]{1,0:T(8,128)S(1)} %get-tuple-element.211, bf16[4,128,8,128]{3,1,2,0:T(8,128)(2,1)S(1)} %get-tuple-element.246, s32[]{:T(128)} %get-tuple-element.237, bf16[2048,1024]{1,0:T(8,128)(2,1)} %get-tuple-element.247), kind=kOutput, calls=%fused_computation.20.clone.1 | convolution fusion | flops 545243136 | bytes 4530180 | tf_op jit(solution)/shard_map/while/body/eval_jaxpr/thd,nhd->htn/dot_general | solution.py:35
  100.1 16.3 %gather_fusion.3 = f32[2048]{0:T(1024)S(1)} fusion(f32[4,8,2048]{2,1,0:T(8,128)S(1)} %get-tuple-element.60, s32[2048]{0:T(1024)S(1)} %reshape.253), kind=kCustom, calls=%fused_computation.3 | custom fusion | bytes 40960 | tf_op jit(solution)/shard_map/jit(take_along_axis)/gather | solution.py:79
  116.4 32.7 %all-to-all-done.1 = bf16[32,64,1024]{2,1,0:T(8,128)(2,1)} async-done(((bf16[32,64,1024]{2,1,0:T(8,128)(2,1)}), bf16[32,64,1024]{2,1,0:T(8,128)(2,1)}, u32[]{:S(2)}, u32[]{:S(2)}) %all-to-all-start.1) | async-done | bytes 4194336 | tf_op jit(solution)/shard_map/all_to_all | solution.py:76
  149.1 4.3 %gather_fusion.1 = bf16[256,1024]{1,0:T(8,128)(2,1)S(1)} fusion(bf16[2048,1024]{1,0:T(8,128)(2,1)} %bitcast.13, s32[1024]{0:T(1024)S(1)} %pad_clamp_fusion), kind=kCustom, calls=%fused_computation.1 | custom fusion | bytes 1049600 | tf_op jit(solution)/shard_map/jit(_take)/gather | solution.py:77
  (63 shorter events, 8.0 us)
Async XLA Ops:
  7.2 25.7 %copy-start = (bf16[512,1024]{1,0:T(8,128)(2,1)S(1)}, bf16[512,1024]{1,0:T(8,128)(2,1)}, u32[]{:S(2)}) copy-start(bf16[512,1024]{1,0:T(8,128)(2,1)} %param.11) | copy-start | bytes 3145732
  7.2 45.5 %all-gather.2.cloned.1.call-start = ((), (), s32[]{:S(2)}) async-start(), calls=%async_computation.2 | async-start | bytes 4718592 | tf_op jit(solution)/shard_map/all_gather | solution.py:41
  14.7 18.0 %all-to-all-start = ((s32[32,1,64]{2,1,0:T(1,128)}), s32[32,1,64]{2,1,0:T(1,128)S(1)}, u32[]{:S(2)}, u32[]{:S(2)}) async-start(s32[32,1,64]{2,1,0:T(1,128)} %sub.59), calls=%async_computation | async-start | bytes 32768 | tf_op jit(solution)/shard_map/all_to_all | solution.py:72
  46.5 102.7 %all-to-all-start.1 = ((bf16[32,64,1024]{2,1,0:T(8,128)(2,1)}), bf16[32,64,1024]{2,1,0:T(8,128)(2,1)}, u32[]{:S(2)}, u32[]{:S(2)}) async-start(bf16[32,64,1024]{2,1,0:T(8,128)(2,1)} %broadcast_select_fusion), calls=%async_computation.1 | async-start | bytes 8388608 | tf_op jit(solution)/shard_map/all_to_all | solution.py:76
  100.1 16.3 %copy-start.1 = (f32[4,8,2048]{2,1,0:T(8,128)}, f32[4,8,2048]{2,1,0:T(8,128)S(1)}, u32[]{:S(2)}) copy-start(f32[4,8,2048]{2,1,0:T(8,128)S(1)} %get-tuple-element.60) | copy-start | bytes 786436
Sparse Core Ops, SparseCore 0:
  9.8 37.9 all-gather.1
where the time goes:
time: 162 us
  matrix products  41.1 us (25%)
  waiting for transfers between devices  37.7 us (23%)
  local copies, waits for them, and re-layouts  37.4 us (23%)
  starting transfers between devices  17.2 us (11%)
  between operations  14.2 us (9%)
  other arithmetic  13.8 us (9%)
    dot_general x8, matrix products, block_scores(): jnp.einsum('thd,nhd->htn', query_block, keyed, preferred_element_type=jnp...  40.3 us
    all_to_all x1, waiting for transfers between devices, per_device(): lax.all_to_all(found, 'col', split_axis=0, concat_axis=0, tiled=True)  32.7 us
    gather x3, local copies, waits for them, and re-layouts, per_device(): jnp.take_along_axis(portion, jnp.broadcast_to(parents[:, None, :], (block...  16.4 us
    all_to_all x1, starting transfers between devices, per_device(): lax.all_to_all(outgoing, 'col', split_axis=0, concat_axis=0, tiled=True)  11 us
    gather x1, local copies, waits for them, and re-layouts, per_device(): jnp.take(fine_keys, jnp.clip(lax.all_to_all(outgoing, 'col', split_axis=0...  9.68 us
    reduce_sum x4, other arithmetic, stat_per_block(): jnp.sum(jnp.exp(scores - new_max[..., None]), axis=-1)  6.58 us
    all_to_all x1, starting transfers between devices, per_device(): lax.all_to_all(found, 'col', split_axis=0, concat_axis=0, tiled=True)  6.19 us
    all_to_all x1, waiting for transfers between devices, per_device(): lax.all_to_all(outgoing, 'col', split_axis=0, concat_axis=0, tiled=True)  4.32 us
  transfers between devices with their start and end apart: 3, of which 2 were waited for; matrix products, arithmetic and copies ran while one was open for 53% of the time, Pallas kernels for 0%

commit v1 on v0

v1 whole, which is shorter than its diff:
```python
import functools
import math

import jax
import jax.numpy as jnp
from jax import lax
from jax.experimental import pallas as pl
from jax.experimental.pallas import tpu as pltpu
from jax.sharding import PartitionSpec as P

H = 8
D = 128
SBLK = 8
PICK = 64
NSEL = 16
LOG2E = 1.4426950408889634

K, X, Y, Z = 2, 4, 4, 8
G = 2 * Y
SUB = 32
STEPS = 14


def kernel(
    q_ref, ck_ref, fk_ref, sid_ref, pk_ref,
    imp_ref, sel_ref,
    table, ck, qb, s_buf, idv, pkv, ids, res, irecv, fres, frecv,
    cs, cr, cds, cdr, qs, qr, ns, nr, ms, mr, xs, xr,
    rs, rr, ls, lr, ds, dr, os_, or_, fs, fr, loc,
):
    NB, T, _ = q_ref.shape
    S = Y * K * ck_ref.shape[0]
    CH = ck_ref.shape[0]
    factor = LOG2E / math.sqrt(D)
    row = lax.axis_index("row")
    col = lax.axis_index("col")
    y, k = row // K, row % K
    z, x = col // X, col % X
    par = x % 2
    me = 2 * y + par

    def at(yy, kk, zz, xx):
        return {"row": yy * K + kk, "col": zz * X + xx}

    def remote(src, dst, send, recv, dev):
        return pltpu.make_async_remote_copy(
            src_ref=src, dst_ref=dst, send_sem=send, recv_sem=recv,
            device_id=dev, device_id_type=pl.DeviceIdType.MESH,
        )

    def arrived(dst, sem):
        pltpu.make_async_copy(dst, dst, sem).wait()

    def peer(n):
        m = n // 2
        yy = (y + m + (m // 2) * (1 - 2 * (m % 2))) % Y
        pp = (par + n) % 2
        return 2 * yy + pp, at(yy, k, z, (x // 2) * 2 + pp)

    def heads(h):
        return pl.ds(pl.multiple_of(h * D, D), D)

    def piece(zz, xx, kk):
        return table.at[pl.ds((zz * X + xx) * (K * SUB) + kk * SUB, SUB)]

    def ck_slot(yy, kk):
        return ck.at[yy * K + kk]

    partner = at(y, 1 - k, z, x)
    right, left = at(y, k, (z + 1) % Z, x), at(y, k, (z + Z - 1) % Z, x)

    greet = [peer(n)[1] for n in range(1, G)]
    greet += [at(y, k, z, (x + 2) % X), at(y, k, z, (x + X - 1 + 2 * par) % X)]
    greet += [right, left, partner]
    barrier = pltpu.get_barrier_semaphore()
    for dev in greet:
        pl.semaphore_signal(barrier, inc=1, device_id=dev, device_id_type=pl.DeviceIdType.MESH)
    pl.semaphore_wait(barrier, len(greet))

    out = []
    for i in range(1, Y):
        yy = (y + i) % Y
        c = remote(ck_ref.at[:, heads(2 * yy + par)], ck_slot(y, k), cs.at[i - 1], cr.at[i - 1],
                   at(yy, k, z, x))
        c.start()
        out.append(c)
    own = fk_ref.at[pl.ds(k * SUB, SUB), :, heads(me)]
    mine = piece(z, x, k)
    remote(own, mine, rs, rr.at[0], right).start()
    remote(own, mine, ls, lr.at[0], left).start()
    for i in range(1, X):
        xx = (x + X - i) % X
        c = remote(fk_ref.at[pl.ds(k * SUB, SUB), :, heads(2 * y + xx % 2)], mine,
                   xs.at[i - 1], xr.at[i - 1], at(y, k, z, xx))
        c.start()
        out.append(c)
    c = remote(ck_ref.at[:, heads(me)], ck_slot(y, k), cds.at[0], cdr.at[0], partner)
    c.start()
    out.append(c)
    remote(own, mine, ds, dr, partner).start()
    local = [
        pltpu.make_async_copy(ck_ref.at[:, heads(me)], ck_slot(y, k), loc.at[0]),
        pltpu.make_async_copy(q_ref.at[:, :, heads(me)], qb.at[me], loc.at[1]),
        pltpu.make_async_copy(own, mine, loc.at[2]),
        pltpu.make_async_copy(sid_ref, idv.at[me], loc.at[3]),
        pltpu.make_async_copy(pk_ref, pkv.at[me], loc.at[4]),
    ]
    for c in local:
        c.start()
    for n in range(1, G):
        g, dev = peer(n)
        for c in (
            remote(q_ref.at[:, :, heads(g)], qb.at[me], qs.at[n - 1], qr.at[me], dev),
            remote(sid_ref, idv.at[me], ns.at[n - 1], nr.at[me], dev),
            remote(pk_ref, pkv.at[me], ms.at[n - 1], mr.at[me], dev),
        ):
            c.start()
            out.append(c)

    for s in range(1, X):
        p = piece(z, (x + s) % X, k)
        arrived(p, xr.at[s - 1])
        remote(p, p, rs, rr.at[s], right).start()
        remote(p, p, ls, lr.at[s], left).start()
        remote(p, p, ds, dr, partner).start()

    def ring(i):
        d = i // X + 1
        sub = i % X
        p = piece((z + Z - d) % Z, (x + sub) % X, k)
        arrived(p, rr.at[i])

        @pl.when(i < STEPS - X)
        def _():
            remote(p, p, rs, rr.at[i + X], right).start()

        remote(p, p, ds, dr, partner).start()
        o = piece((z + d) % Z, (x + sub + 2 * (i // (3 * X))) % X, k)
        arrived(o, lr.at[i])

        @pl.when(i < 2 * X)
        def _():
            remote(o, o, ls, lr.at[i + X], left).start()

        @pl.when((i >= STEPS - X) & (i < 3 * X))
        def _():
            remote(o, o, ls, lr.at[i + 2], left).start()

        remote(o, o, ds, dr, partner).start()

    def wait_queries(n):
        g, _ = peer(n)
        arrived(qb.at[g], qr.at[g])

    def dots(u):
        g, _ = peer(u // NB)
        qq = qb[g, u % NB]
        for r in range(Y * K):
            s_buf[u % 2, :, r * CH:(r + 1) * CH] = lax.dot_general(
                qq, ck[r], (((1,), (1,)), ((), ())), preferred_element_type=jnp.float32
            )

    def soften(u):
        g, _ = peer(u // NB)
        b = u % NB
        acc = jnp.zeros((8, S), jnp.float32)
        for t in range(T // 8):
            sc = s_buf[u % 2, t * 8:(t + 1) * 8, :]
            top = jnp.max(sc, axis=1, keepdims=True)
            e = jnp.exp2(sc * factor - top * factor)
            acc = acc + e * (1.0 / jnp.sum(e, axis=1, keepdims=True))
        total = jnp.sum(acc, axis=0, keepdims=True) * (S / T)
        for j in range(S // D):
            res[g, b, j:j + 1, :] = total[:, j * D:(j + 1) * D]

    def send_importance(n):
        g, dev = peer(n)
        return remote(res.at[g], irecv.at[me], os_.at[n], or_.at[me], dev)

    def block(u, carry):
        nxt = jnp.minimum(u + 1, G * NB - 1)

        @pl.when((u % NB == NB - 1) & (u < (G - 1) * NB))
        def _():
            wait_queries(nxt // NB)

        @pl.when((u % NB == 0) & (u >= 3 * NB))
        def _():
            send_importance(u // NB - 2).start()

        dots(nxt)
        soften(u)
        return carry

    ring(0)
    for i in range(1, Y):
        slot = ck_slot((y + Y - i) % Y, k)
        arrived(slot, cr.at[i - 1])
        c = remote(slot, slot, cds.at[i], cdr.at[i], partner)
        c.start()
        out.append(c)
    local[0].wait()
    for i in range(Y):
        arrived(ck_slot((y + Y - i) % Y, 1 - k), cdr.at[i])
    local[1].wait()
    dots(0)

    def tick(i, carry):
        ring(i)
        lax.fori_loop(jnp.minimum(3 * (i - 1), G * NB), jnp.minimum(3 * i, G * NB), block, 0)
        return carry

    lax.fori_loop(1, STEPS, tick, 0)
    for n in (G - 2, G - 1):
        send_importance(n).start()

    for n in range(1, G):
        g, _ = peer(n)
        arrived(idv.at[g], nr.at[g])
        arrived(pkv.at[g], mr.at[g])
    for c in local[2:]:
        c.wait()
    to_smem = pltpu.make_async_copy(idv, ids, loc.at[5])
    to_smem.start()
    to_smem.wait()
    half = table.at[pl.ds(0, table.shape[0] // 2)]
    arrived(half, dr)

    def send_picked(n):
        g, dev = peer(n)
        return remote(fres.at[g], frecv.at[me], fs.at[n], fr.at[me], dev)

    place = lax.broadcasted_iota(jnp.int32, (NSEL * SBLK, PICK), 0)

    def fine(n):
        g, _ = peer(n)
        for b in range(NB):
            rows = [table[ids[g, b, s]].astype(jnp.float32) for s in range(NSEL)]
            cand = jnp.concatenate(rows, axis=0).astype(jnp.bfloat16)
            sc = lax.dot_general(
                cand, qb[g, b], (((1,), (1,)), ((), ())), preferred_element_type=jnp.float32
            )
            hit = (place == pkv[g, b:b + 1, :]).astype(jnp.float32)
            picked = jnp.max(hit, axis=1, keepdims=True) > 0.0
            sc = jnp.where(picked, sc * factor, -1e30)
            top = jnp.max(sc, axis=0, keepdims=True)
            e = jnp.exp2(sc - top)
            e = e * (1.0 / jnp.sum(e, axis=0, keepdims=True))
            val = jnp.sum(e, axis=1, keepdims=True)
            fres[g, b:b + 1, :] = jnp.sum(hit * val, axis=0, keepdims=True)

    def fine_step(n, carry):
        @pl.when(n > 1)
        def _():
            send_picked(n - 1).start()

        fine(n)
        return carry

    lax.fori_loop(1, G, fine_step, 0)
    fine(0)
    send_picked(G - 1).start()
    frecv[me] = fres[me]
    irecv[me] = res[me]

    for n in range(1, G):
        g, _ = peer(n)
        arrived(irecv.at[g], or_.at[g])
    for b in range(NB):
        for j in range(S // D):
            imp_ref[b, j] = irecv[:, b, j, :]
    lane = lax.broadcasted_iota(jnp.int32, (H, D), 1)
    weights = []
    for b in range(NB):
        owner = lax.shift_right_logical(pkv[me, b:b + 1, :], 3)
        w = jnp.zeros((H, PICK), jnp.float32)
        for s in range(NSEL):
            sid = ids[me, b, s]
            part = imp_ref[b, lax.shift_right_logical(sid, 7)]
            one = jnp.sum(jnp.where(lane == (sid & (D - 1)), part, 0.0), axis=1, keepdims=True)
            w = w + jnp.where(owner == s, one, 0.0)
        weights.append(w * (PICK / T))
    for n in range(1, G):
        g, _ = peer(n)
        arrived(frecv.at[g], fr.at[g])
    for b in range(NB):
        sel_ref[b] = frecv[:, b, :] * weights[b]

    for c in out:
        c.wait_send()
    for n in range(1, G):
        send_importance(n).wait_send()
        send_picked(n).wait_send()
    arrived(table.at[pl.ds(0, STEPS * SUB)], rs)
    arrived(table.at[pl.ds(0, STEPS * SUB)], ls)
    arrived(half, ds)


def per_device(queries, coarse_keys, fine_keys, super_ids, picks):
    nb, t, width = queries.shape
    ch = coarse_keys.shape[0]
    s = ch * Y * K
    dma = pltpu.SemaphoreType.DMA
    f32, bf16, i32 = jnp.float32, jnp.bfloat16, jnp.int32
    imp, sel = pl.pallas_call(
        kernel,
        out_shape=(
            jax.ShapeDtypeStruct((nb, s // D, H, D), f32),
            jax.ShapeDtypeStruct((nb, H, PICK), f32),
        ),
        in_specs=[pl.BlockSpec(memory_space=pl.ANY)] * 5,
        out_specs=[pl.BlockSpec(memory_space=pltpu.VMEM)] * 2,
        scratch_shapes=[
            pltpu.VMEM((s, SBLK, D), bf16),
            pltpu.VMEM((Y * K, ch, D), bf16),
            pltpu.VMEM((G, nb, t, D), bf16),
            pltpu.VMEM((2, t, s), f32),
            pltpu.VMEM((G, nb, NSEL), i32),
            pltpu.VMEM((G, nb, PICK), i32),
            pltpu.SMEM((G, nb, NSEL), i32),
            pltpu.VMEM((G, nb, s // D, D), f32),
            pltpu.VMEM((G, nb, s // D, D), f32),
            pltpu.VMEM((G, nb, PICK), f32),
            pltpu.VMEM((G, nb, PICK), f32),
            dma((Y - 1,)), dma((Y - 1,)), dma((Y,)), dma((Y,)),
            dma((G - 1,)), dma((G,)), dma((G - 1,)), dma((G,)), dma((G - 1,)), dma((G,)),
            dma((X - 1,)), dma((X - 1,)),
            dma, dma((STEPS,)), dma, dma((STEPS,)), dma, dma,
            dma((G,)), dma((G,)), dma((G,)), dma((G,)), dma((6,)),
        ],
        compiler_params=pltpu.CompilerParams(collective_id=0, has_side_effects=True),
    )(queries, coarse_keys, fine_keys.reshape(-1, SBLK, width), super_ids, picks)
    return imp.transpose(0, 2, 1, 3).reshape(nb, H, s), sel.reshape(nb, H * PICK)


def solution(mesh):
    return jax.shard_map(
        per_device,
        mesh=mesh,
        in_specs=(
            P(("row", "col"), None, None),
            P("row", None),
            P("col", None),
            P(("row", "col"), None),
            P(("row", "col"), None),
        ),
        out_specs=(P(("row", "col"), None, None), P(("row", "col"), None)),
        check_vma=False,
    )
```

time: 162 us -> 56.7 us (0.35)
  the two profiles are of different devices: /device:TPU:7 before, /device:TPU:1 now
where the time goes in v1:
time: 56.7 us; the launch traced here: 56.5 us
  Pallas kernels  52.8 us (93%)
  local copies, waits for them, and re-layouts  3.06 us (5%)
  between operations  0.64 us (1%)
    pallas_call x1, Pallas kernels, per_device(): pl.pallas_call(kernel, out_shape=(jax.ShapeDtypeStruct((nb, s // D, H, D)...  52.8 us
    unnamed x1, local copies, waits for them, and re-layouts  1.67 us
    reshape x1, local copies, waits for them, and re-layouts, per_device(): sel.reshape(nb, H * PICK)  1.39 us

profile of v1, /device:TPU:1, one launch (start us, length us, event | category | flops | bytes accessed | tf_op | source)
XLA Modules:
  0.0 56.5 jit_solution(13193380358583073454)
XLA Ops:
  0.6 52.8 %shard_map.68 = (f32[4,16,8,128]{3,2,1,0:T(8,128)}, f32[4,8,64]{2,1,0:T(8,128)}) custom-call(bf16[4,128,1024]{2,1,0:T(8,128)(2,1)} %q_ref.1, bf16[256,1024]{1,0:T(8,128)(2,1)} %ck_ref.1, bf16[64,8,1024]{2,1,0:T(8,128)(2,1)} %bitcast.4, s32[4,16]{1,0:T(4,128)} %sid_ref.1, s32[4,64]{1,0:T(4,128)} %pk_ref.1), custom_call_target="tpu_custom_call" | custom-call | tf_op jit(solution)/shard_map/pallas_call | solution.py:305
  53.5 1.4 %reshape.15 = f32[4,512]{1,0:T(4,128)} reshape(f32[4,8,64]{2,1,0:T(8,128)} %get-tuple-element.5) | data formatting | bytes 16384 | tf_op jit(solution)/shard_map/reshape | solution.py:333
  54.9 1.7 %copy.8 = f32[4,8,2048]{2,1,0:T(8,128)} copy(f32[4,8,2048]{2,1,0:T(8,128)} %bitcast.5) | data formatting | bytes 524288

commit v2 on v1

--- a/solution.py
+++ b/solution.py
@@ -24,13 +24,14 @@
 def kernel(
     q_ref, ck_ref, fk_ref, sid_ref, pk_ref,
     imp_ref, sel_ref,
-    table, ck, qb, s_buf, idv, pkv, ids, res, irecv, fres, frecv,
+    table, ck, qb, s_even, s_odd, e_buf, idv, pkv, ids, res, irecv, fres, frecv,
     cs, cr, cds, cdr, qs, qr, ns, nr, ms, mr, xs, xr,
     rs, rr, ls, lr, ds, dr, os_, or_, fs, fr, loc,
 ):
     NB, T, _ = q_ref.shape
     S = Y * K * ck_ref.shape[0]
     CH = ck_ref.shape[0]
+    PER = Y * K // NB
     factor = LOG2E / math.sqrt(D)
     row = lax.axis_index("row")
     col = lax.axis_index("col")
@@ -152,44 +153,58 @@
         g, _ = peer(n)
         arrived(qb.at[g], qr.at[g])
 
-    def dots(u):
-        g, _ = peer(u // NB)
-        qq = qb[g, u % NB]
-        for r in range(Y * K):
-            s_buf[u % 2, :, r * CH:(r + 1) * CH] = lax.dot_general(
-                qq, ck[r], (((1,), (1,)), ((), ())), preferred_element_type=jnp.float32
+    def dots(n, s_buf, c):
+        g, _ = peer(n)
+        qq = qb[g].reshape(NB * T, D)
+        for r in range(PER):
+            sc = lax.dot_general(
+                qq, ck[c * PER + r], (((1,), (1,)), ((), ())), preferred_element_type=jnp.float32
             )
-
-    def soften(u):
-        g, _ = peer(u // NB)
-        b = u % NB
-        acc = jnp.zeros((8, S), jnp.float32)
-        for t in range(T // 8):
-            sc = s_buf[u % 2, t * 8:(t + 1) * 8, :]
-            top = jnp.max(sc, axis=1, keepdims=True)
-            e = jnp.exp2(sc * factor - top * factor)
-            acc = acc + e * (1.0 / jnp.sum(e, axis=1, keepdims=True))
-        total = jnp.sum(acc, axis=0, keepdims=True) * (S / T)
+            for j in range(CH // D):
+                s_buf[(c * PER + r) * (CH // D) + j] = sc[:, j * D:(j + 1) * D]
+
+    def soften(n, s_buf, b):
+        g, _ = peer(n)
+        rows = pl.ds(pl.multiple_of(b * T, T), T)
+        top = s_buf[0, rows, :]
+        for j in range(1, S // D):
+            top = jnp.maximum(top, s_buf[j, rows, :])
+        top = jnp.max(top, axis=1, keepdims=True) * factor
+        z = None
         for j in range(S // D):
-            res[g, b, j:j + 1, :] = total[:, j * D:(j + 1) * D]
+            e = jnp.exp2(s_buf[j, rows, :] * factor - top)
+            e_buf[j] = e
+            z = e if z is None else z + e
+        w = (S / T) / jnp.sum(z, axis=1, keepdims=True)
+        for j in range(S // D):
+            res[g, b, j:j + 1, :] = jnp.sum(e_buf[j] * w, axis=0, keepdims=True)
 
     def send_importance(n):
         g, dev = peer(n)
         return remote(res.at[g], irecv.at[me], os_.at[n], or_.at[me], dev)
 
     def block(u, carry):
-        nxt = jnp.minimum(u + 1, G * NB - 1)
-
-        @pl.when((u % NB == NB - 1) & (u < (G - 1) * NB))
-        def _():
-            wait_queries(nxt // NB)
-
-        @pl.when((u % NB == 0) & (u >= 3 * NB))
-        def _():
-            send_importance(u // NB - 2).start()
-
-        dots(nxt)
-        soften(u)
+        n, b = u // NB, u % NB
+        nxt = jnp.minimum(n + 1, G - 1)
+
+        @pl.when((b == 0) & (n < G - 1))
+        def _():
+            wait_queries(nxt)
+
+        @pl.when((b == 0) & (n >= 3))
+        def _():
+            send_importance(n - 2).start()
+
+        @pl.when(n % 2 == 0)
+        def _():
+            dots(nxt, s_odd, b)
+            soften(n, s_even, b)
+
+        @pl.when(n % 2 == 1)
+        def _():
+            dots(nxt, s_even, b)
+            soften(n, s_odd, b)
+
         return carry
 
     ring(0)
@@ -203,7 +218,12 @@
     for i in range(Y):
         arrived(ck_slot((y + Y - i) % Y, 1 - k), cdr.at[i])
     local[1].wait()
-    dots(0)
+
+    def first(c, carry):
+        dots(0, s_even, c)
+        return carry
+
+    lax.fori_loop(0, NB, first, 0)
 
     def tick(i, carry):
         ring(i)
@@ -314,7 +334,9 @@
             pltpu.VMEM((s, SBLK, D), bf16),
             pltpu.VMEM((Y * K, ch, D), bf16),
             pltpu.VMEM((G, nb, t, D), bf16),
-            pltpu.VMEM((2, t, s), f32),
+            pltpu.VMEM((s // D, nb * t, D), f32),
+            pltpu.VMEM((s // D, nb * t, D), f32),
+            pltpu.VMEM((s // D, t, D), f32),
             pltpu.VMEM((G, nb, NSEL), i32),
             pltpu.VMEM((G, nb, PICK), i32),
             pltpu.SMEM((G, nb, NSEL), i32),

time: 56.7 us -> 50 us (0.88)
  Pallas kernels: 52.8 us -> 46.1 us
    pallas_call x1, Pallas kernels: 52.8 us -> 46.1 us  [per_device(): pl.pallas_call(kernel, out_shape=(jax.ShapeDtypeStruct((nb, s // D, H, D)...]
where the time goes in v2:
time: 50 us; the launch traced here: 49.8 us
  Pallas kernels  46.1 us (92%)
  local copies, waits for them, and re-layouts  3.06 us (6%)
  between operations  0.64 us (1%)
    pallas_call x1, Pallas kernels, per_device(): pl.pallas_call(kernel, out_shape=(jax.ShapeDtypeStruct((nb, s // D, H, D)...  46.1 us
    unnamed x1, local copies, waits for them, and re-layouts  1.67 us
    reshape x1, local copies, waits for them, and re-layouts, per_device(): sel.reshape(nb, H * PICK)  1.39 us

profile of v2, /device:TPU:1, one launch (start us, length us, event | category | flops | bytes accessed | tf_op | source)
XLA Modules:
  0.0 49.8 jit_solution(6073963514184745952)
XLA Ops:
  0.6 46.1 %shard_map.68 = (f32[4,16,8,128]{3,2,1,0:T(8,128)}, f32[4,8,64]{2,1,0:T(8,128)}) custom-call(bf16[4,128,1024]{2,1,0:T(8,128)(2,1)} %q_ref.1, bf16[256,1024]{1,0:T(8,128)(2,1)} %ck_ref.1, bf16[64,8,1024]{2,1,0:T(8,128)(2,1)} %bitcast.4, s32[4,16]{1,0:T(4,128)} %sid_ref.1, s32[4,64]{1,0:T(4,128)} %pk_ref.1), custom_call_target="tpu_custom_call" | custom-call | tf_op jit(solution)/shard_map/pallas_call | solution.py:325
  46.7 1.4 %reshape.15 = f32[4,512]{1,0:T(4,128)} reshape(f32[4,8,64]{2,1,0:T(8,128)} %get-tuple-element.5) | data formatting | bytes 16384 | tf_op jit(solution)/shard_map/reshape | solution.py:355
  48.1 1.7 %copy.8 = f32[4,8,2048]{2,1,0:T(8,128)} copy(f32[4,8,2048]{2,1,0:T(8,128)} %bitcast.5) | data formatting | bytes 524288

commit v3 on v2

--- a/solution.py
+++ b/solution.py
@@ -24,7 +24,7 @@
 def kernel(
     q_ref, ck_ref, fk_ref, sid_ref, pk_ref,
     imp_ref, sel_ref,
-    table, ck, qb, s_even, s_odd, e_buf, idv, pkv, ids, res, irecv, fres, frecv,
+    table, ck, qb, s_even, s_odd, e_buf, idv, pkv, ids, res, irecv, fres, frecv, bias,
     cs, cr, cds, cdr, qs, qr, ns, nr, ms, mr, xs, xr,
     rs, rr, ls, lr, ds, dr, os_, or_, fs, fr, loc,
 ):
@@ -111,12 +111,16 @@
     for n in range(1, G):
         g, dev = peer(n)
         for c in (
-            remote(q_ref.at[:, :, heads(g)], qb.at[me], qs.at[n - 1], qr.at[me], dev),
             remote(sid_ref, idv.at[me], ns.at[n - 1], nr.at[me], dev),
             remote(pk_ref, pkv.at[me], ms.at[n - 1], mr.at[me], dev),
         ):
             c.start()
             out.append(c)
+    for n in range(1, G):
+        g, dev = peer(n)
+        c = remote(q_ref.at[:, :, heads(g)], qb.at[me], qs.at[n - 1], qr.at[me], dev)
+        c.start()
+        out.append(c)
 
     for s in range(1, X):
         p = piece(z, (x + s) % X, k)
@@ -214,6 +218,33 @@
         c = remote(slot, slot, cds.at[i], cdr.at[i], partner)
         c.start()
         out.append(c)
+    place = lax.broadcasted_iota(jnp.int32, (NSEL * SBLK, 2 * PICK), 0)
+    mine_half = lax.broadcasted_iota(jnp.int32, (1, 2 * PICK), 1) // PICK == par
+
+    def hits(g, b):
+        row = jnp.concatenate([pkv[g, b:b + 1, :]] * 2, axis=1)
+        return place == jnp.where(mine_half, row, -1)
+
+    def masks():
+        for n in range(1, G):
+            g, _ = peer(n)
+            arrived(idv.at[g], nr.at[g])
+            arrived(pkv.at[g], mr.at[g])
+        for c in local[2:]:
+            c.wait()
+        to_smem = pltpu.make_async_copy(idv, ids, loc.at[5])
+        to_smem.start()
+
+        def one(g, carry):
+            for b in range(NB):
+                found = jnp.max(hits(g, b).astype(jnp.float32), axis=1, keepdims=True)
+                bias[g, b] = jnp.broadcast_to(jnp.where(found > 0.0, 0.0, -1e30), (NSEL * SBLK, T))
+            return carry
+
+        lax.fori_loop(0, G, one, 0)
+        to_smem.wait()
+
+    masks()
     local[0].wait()
     for i in range(Y):
         arrived(ck_slot((y + Y - i) % Y, 1 - k), cdr.at[i])
@@ -234,23 +265,12 @@
     for n in (G - 2, G - 1):
         send_importance(n).start()
 
-    for n in range(1, G):
-        g, _ = peer(n)
-        arrived(idv.at[g], nr.at[g])
-        arrived(pkv.at[g], mr.at[g])
-    for c in local[2:]:
-        c.wait()
-    to_smem = pltpu.make_async_copy(idv, ids, loc.at[5])
-    to_smem.start()
-    to_smem.wait()
     half = table.at[pl.ds(0, table.shape[0] // 2)]
     arrived(half, dr)
 
     def send_picked(n):
         g, dev = peer(n)
         return remote(fres.at[g], frecv.at[me], fs.at[n], fr.at[me], dev)
-
-    place = lax.broadcasted_iota(jnp.int32, (NSEL * SBLK, PICK), 0)
 
     def fine(n):
         g, _ = peer(n)
@@ -260,26 +280,26 @@
             sc = lax.dot_general(
                 cand, qb[g, b], (((1,), (1,)), ((), ())), preferred_element_type=jnp.float32
             )
-            hit = (place == pkv[g, b:b + 1, :]).astype(jnp.float32)
-            picked = jnp.max(hit, axis=1, keepdims=True) > 0.0
-            sc = jnp.where(picked, sc * factor, -1e30)
+            sc = sc * factor + bias[g, b]
             top = jnp.max(sc, axis=0, keepdims=True)
             e = jnp.exp2(sc - top)
             e = e * (1.0 / jnp.sum(e, axis=0, keepdims=True))
             val = jnp.sum(e, axis=1, keepdims=True)
-            fres[g, b:b + 1, :] = jnp.sum(hit * val, axis=0, keepdims=True)
+            fres[g, b:b + 1, :] = jnp.sum(jnp.where(hits(g, b), val, 0.0), axis=0, keepdims=True)
 
     def fine_step(n, carry):
+        m = G - n
+
         @pl.when(n > 1)
         def _():
-            send_picked(n - 1).start()
-
-        fine(n)
+            send_picked(m + 1).start()
+
+        fine(m)
         return carry
 
     lax.fori_loop(1, G, fine_step, 0)
     fine(0)
-    send_picked(G - 1).start()
+    send_picked(1).start()
     frecv[me] = fres[me]
     irecv[me] = res[me]
 
@@ -292,8 +312,8 @@
     lane = lax.broadcasted_iota(jnp.int32, (H, D), 1)
     weights = []
     for b in range(NB):
-        owner = lax.shift_right_logical(pkv[me, b:b + 1, :], 3)
-        w = jnp.zeros((H, PICK), jnp.float32)
+        owner = lax.shift_right_logical(jnp.concatenate([pkv[me, b:b + 1, :]] * 2, axis=1), 3)
+        w = jnp.zeros((H, 2 * PICK), jnp.float32)
         for s in range(NSEL):
             sid = ids[me, b, s]
             part = imp_ref[b, lax.shift_right_logical(sid, 7)]
@@ -304,7 +324,9 @@
         g, _ = peer(n)
         arrived(frecv.at[g], fr.at[g])
     for b in range(NB):
-        sel_ref[b] = frecv[:, b, :] * weights[b]
+        both = frecv[:, b, :] * weights[b]
+        for h in range(0, H, 2):
+            sel_ref[b:b + 1, h * PICK:(h + 2) * PICK] = both[h:h + 1] + both[h + 1:h + 2]
 
     for c in out:
         c.wait_send()
@@ -326,7 +348,7 @@
         kernel,
         out_shape=(
             jax.ShapeDtypeStruct((nb, s // D, H, D), f32),
-            jax.ShapeDtypeStruct((nb, H, PICK), f32),
+            jax.ShapeDtypeStruct((nb, H * PICK), f32),
         ),
         in_specs=[pl.BlockSpec(memory_space=pl.ANY)] * 5,
         out_specs=[pl.BlockSpec(memory_space=pltpu.VMEM)] * 2,
@@ -342,8 +364,9 @@
             pltpu.SMEM((G, nb, NSEL), i32),
             pltpu.VMEM((G, nb, s // D, D), f32),
             pltpu.VMEM((G, nb, s // D, D), f32),
-            pltpu.VMEM((G, nb, PICK), f32),
-            pltpu.VMEM((G, nb, PICK), f32),
+            pltpu.VMEM((G, nb, 2 * PICK), f32),
+            pltpu.VMEM((G, nb, 2 * PICK), f32),
+            pltpu.VMEM((G, nb, NSEL * SBLK, t), f32),
             dma((Y - 1,)), dma((Y - 1,)), dma((Y,)), dma((Y,)),
             dma((G - 1,)), dma((G,)), dma((G - 1,)), dma((G,)), dma((G - 1,)), dma((G,)),
             dma((X - 1,)), dma((X - 1,)),
@@ -352,7 +375,7 @@
         ],
         compiler_params=pltpu.CompilerParams(collective_id=0, has_side_effects=True),
     )(queries, coarse_keys, fine_keys.reshape(-1, SBLK, width), super_ids, picks)
-    return imp.transpose(0, 2, 1, 3).reshape(nb, H, s), sel.reshape(nb, H * PICK)
+    return imp.transpose(0, 2, 1, 3).reshape(nb, H, s), sel
 
 
 def solution(mesh):

time: 50 us -> 48 us (0.960)
  Pallas kernels: 46.1 us -> 45 us
  local copies, waits for them, and re-layouts: 3.06 us -> 2.28 us
    reshape x1 -> x0, local copies, waits for them, and re-layouts: 1.39 us -> none  [per_device(): sel.reshape(nb, H * PICK)]
    pallas_call x1, Pallas kernels: 46.1 us -> 45 us  [per_device(): pl.pallas_call(kernel, out_shape=(jax.ShapeDtypeStruct((nb, s // D, H, D)...]
    unnamed x1 -> x4, local copies, waits for them, and re-layouts: 1.67 us -> 2.28 us
where the time goes in v3:
time: 48 us; the launch traced here: 47.9 us
  Pallas kernels  45 us (94%)
  local copies, waits for them, and re-layouts  2.28 us (5%)
  between operations  0.65 us (1%)
    pallas_call x1, Pallas kernels, per_device(): pl.pallas_call(kernel, out_shape=(jax.ShapeDtypeStruct((nb, s // D, H, D)...  45 us
    unnamed x4, local copies, waits for them, and re-layouts  2.28 us

profile of v3, /device:TPU:1, one launch (start us, length us, event | category | flops | bytes accessed | tf_op | source)
XLA Modules:
  0.0 47.9 jit_solution(13916951261176582530)
XLA Ops:
  0.6 45.0 %shard_map.68 = (f32[4,16,8,128]{3,2,1,0:T(8,128)}, f32[4,512]{1,0:T(4,128)}) custom-call(bf16[4,128,1024]{2,1,0:T(8,128)(2,1)} %q_ref.1, bf16[256,1024]{1,0:T(8,128)(2,1)} %ck_ref.1, bf16[64,8,1024]{2,1,0:T(8,128)(2,1)} %bitcast.4, s32[4,16]{1,0:T(4,128)} %sid_ref.1, s32[4,64]{1,0:T(4,128)} %pk_ref.1), custom_call_target="tpu_custom_call" | custom-call | tf_op jit(solution)/shard_map/pallas_call | solution.py:347
  45.6 0.0 copy-start
  45.6 1.7 %copy.9 = f32[4,8,2048]{2,1,0:T(8,128)} copy(f32[4,8,2048]{2,1,0:T(8,128)} %bitcast.5) | data formatting | bytes 524288
  47.3 0.0 copy-done
  47.3 0.6 %copy.10 = f32[4,512]{1,0:T(4,128)} copy(f32[4,512]{1,0:T(4,128)S(1)} %copy-done) | data formatting | bytes 16384
Async XLA Ops:
  45.6 1.7 %copy-start = (f32[4,512]{1,0:T(4,128)S(1)}, f32[4,512]{1,0:T(4,128)}, u32[]{:S(2)}) copy-start(f32[4,512]{1,0:T(4,128)} %get-tuple-element.9) | copy-start | bytes 24580

commit v4 on v3

--- a/solution.py
+++ b/solution.py
@@ -22,10 +22,10 @@
 
 
 def kernel(
-    q_ref, ck_ref, fk_ref, sid_ref, pk_ref,
-    imp_ref, sel_ref,
-    table, ck, qb, s_even, s_odd, e_buf, idv, pkv, ids, res, irecv, fres, frecv, bias,
-    cs, cr, cds, cdr, qs, qr, ns, nr, ms, mr, xs, xr,
+    q_ref, ck_ref, fk_ref, pk_ref,
+    imp_out, sel_ref,
+    table, ck, qb, s_even, s_odd, e_buf, pkv, ids, res, irecv, fres, frecv, bias, imp_ref,
+    cs, cr, cds, cdr, qs, qr, ms, mr, xs, xr,
     rs, rr, ls, lr, ds, dr, os_, or_, fs, fr, loc,
 ):
     NB, T, _ = q_ref.shape
@@ -103,19 +103,15 @@
         pltpu.make_async_copy(ck_ref.at[:, heads(me)], ck_slot(y, k), loc.at[0]),
         pltpu.make_async_copy(q_ref.at[:, :, heads(me)], qb.at[me], loc.at[1]),
         pltpu.make_async_copy(own, mine, loc.at[2]),
-        pltpu.make_async_copy(sid_ref, idv.at[me], loc.at[3]),
         pltpu.make_async_copy(pk_ref, pkv.at[me], loc.at[4]),
     ]
     for c in local:
         c.start()
     for n in range(1, G):
         g, dev = peer(n)
-        for c in (
-            remote(sid_ref, idv.at[me], ns.at[n - 1], nr.at[me], dev),
-            remote(pk_ref, pkv.at[me], ms.at[n - 1], mr.at[me], dev),
-        ):
-            c.start()
-            out.append(c)
+        c = remote(pk_ref, pkv.at[me], ms.at[n - 1], mr.at[me], dev)
+        c.start()
+        out.append(c)
     for n in range(1, G):
         g, dev = peer(n)
         c = remote(q_ref.at[:, :, heads(g)], qb.at[me], qs.at[n - 1], qr.at[me], dev)
@@ -222,17 +218,16 @@
     mine_half = lax.broadcasted_iota(jnp.int32, (1, 2 * PICK), 1) // PICK == par
 
     def hits(g, b):
-        row = jnp.concatenate([pkv[g, b:b + 1, :]] * 2, axis=1)
+        row = jnp.concatenate([pkv[g, b:b + 1, :PICK]] * 2, axis=1)
         return place == jnp.where(mine_half, row, -1)
 
     def masks():
         for n in range(1, G):
             g, _ = peer(n)
-            arrived(idv.at[g], nr.at[g])
             arrived(pkv.at[g], mr.at[g])
         for c in local[2:]:
             c.wait()
-        to_smem = pltpu.make_async_copy(idv, ids, loc.at[5])
+        to_smem = pltpu.make_async_copy(pkv, ids, loc.at[5])
         to_smem.start()
 
         def one(g, carry):
@@ -275,7 +270,7 @@
     def fine(n):
         g, _ = peer(n)
         for b in range(NB):
-            rows = [table[ids[g, b, s]].astype(jnp.float32) for s in range(NSEL)]
+            rows = [table[ids[g, b, PICK + s]].astype(jnp.float32) for s in range(NSEL)]
             cand = jnp.concatenate(rows, axis=0).astype(jnp.bfloat16)
             sc = lax.dot_general(
                 cand, qb[g, b], (((1,), (1,)), ((), ())), preferred_element_type=jnp.float32
@@ -309,13 +304,15 @@
     for b in range(NB):
         for j in range(S // D):
             imp_ref[b, j] = irecv[:, b, j, :]
+    imp_copy = pltpu.make_async_copy(imp_ref, imp_out, loc.at[6])
+    imp_copy.start()
     lane = lax.broadcasted_iota(jnp.int32, (H, D), 1)
     weights = []
     for b in range(NB):
-        owner = lax.shift_right_logical(jnp.concatenate([pkv[me, b:b + 1, :]] * 2, axis=1), 3)
+        owner = lax.shift_right_logical(jnp.concatenate([pkv[me, b:b + 1, :PICK]] * 2, axis=1), 3)
         w = jnp.zeros((H, 2 * PICK), jnp.float32)
         for s in range(NSEL):
-            sid = ids[me, b, s]
+            sid = ids[me, b, PICK + s]
             part = imp_ref[b, lax.shift_right_logical(sid, 7)]
             one = jnp.sum(jnp.where(lane == (sid & (D - 1)), part, 0.0), axis=1, keepdims=True)
             w = w + jnp.where(owner == s, one, 0.0)
@@ -328,6 +325,7 @@
         for h in range(0, H, 2):
             sel_ref[b:b + 1, h * PICK:(h + 2) * PICK] = both[h:h + 1] + both[h + 1:h + 2]
 
+    imp_copy.wait()
     for c in out:
         c.wait_send()
     for n in range(1, G):
@@ -344,14 +342,15 @@
     s = ch * Y * K
     dma = pltpu.SemaphoreType.DMA
     f32, bf16, i32 = jnp.float32, jnp.bfloat16, jnp.int32
+    named = jnp.concatenate([picks, super_ids], axis=1)
     imp, sel = pl.pallas_call(
         kernel,
         out_shape=(
             jax.ShapeDtypeStruct((nb, s // D, H, D), f32),
             jax.ShapeDtypeStruct((nb, H * PICK), f32),
         ),
-        in_specs=[pl.BlockSpec(memory_space=pl.ANY)] * 5,
-        out_specs=[pl.BlockSpec(memory_space=pltpu.VMEM)] * 2,
+        in_specs=[pl.BlockSpec(memory_space=pl.ANY)] * 4,
+        out_specs=[pl.BlockSpec(memory_space=pl.ANY), pl.BlockSpec(memory_space=pltpu.VMEM)],
         scratch_shapes=[
             pltpu.VMEM((s, SBLK, D), bf16),
             pltpu.VMEM((Y * K, ch, D), bf16),
@@ -359,22 +358,22 @@
             pltpu.VMEM((s // D, nb * t, D), f32),
             pltpu.VMEM((s // D, nb * t, D), f32),
             pltpu.VMEM((s // D, t, D), f32),
-            pltpu.VMEM((G, nb, NSEL), i32),
-            pltpu.VMEM((G, nb, PICK), i32),
-            pltpu.SMEM((G, nb, NSEL), i32),
+            pltpu.VMEM((G, nb, PICK + NSEL), i32),
+            pltpu.SMEM((G, nb, PICK + NSEL), i32),
             pltpu.VMEM((G, nb, s // D, D), f32),
             pltpu.VMEM((G, nb, s // D, D), f32),
             pltpu.VMEM((G, nb, 2 * PICK), f32),
             pltpu.VMEM((G, nb, 2 * PICK), f32),
             pltpu.VMEM((G, nb, NSEL * SBLK, t), f32),
+            pltpu.VMEM((nb, s // D, H, D), f32),
             dma((Y - 1,)), dma((Y - 1,)), dma((Y,)), dma((Y,)),
-            dma((G - 1,)), dma((G,)), dma((G - 1,)), dma((G,)), dma((G - 1,)), dma((G,)),
+            dma((G - 1,)), dma((G,)), dma((G - 1,)), dma((G,)),
             dma((X - 1,)), dma((X - 1,)),
             dma, dma((STEPS,)), dma, dma((STEPS,)), dma, dma,
-            dma((G,)), dma((G,)), dma((G,)), dma((G,)), dma((6,)),
+            dma((G,)), dma((G,)), dma((G,)), dma((G,)), dma((7,)),
         ],
-        compiler_params=pltpu.CompilerParams(collective_id=0, has_side_effects=True),
-    )(queries, coarse_keys, fine_keys.reshape(-1, SBLK, width), super_ids, picks)
+        compiler_params=pltpu.CompilerParams(collective_id=0, has_side_effects=True, vmem_limit_bytes=56_000_000),
+    )(queries, coarse_keys, fine_keys.reshape(-1, SBLK, width), named)
     return imp.transpose(0, 2, 1, 3).reshape(nb, H, s), sel
 
 

time: 48 us -> 46.6 us (0.971)
  Pallas kernels: 45 us -> 43.7 us
  local copies, waits for them, and re-layouts: 2.28 us -> 1.3 us
  other arithmetic: 0 us -> 0.77 us
    pallas_call x1, Pallas kernels: 45 us -> 43.7 us  [per_device(): pl.pallas_call(kernel, out_shape=(jax.ShapeDtypeStruct((nb, s // D, H, D)...]
    unnamed x4 -> x2, local copies, waits for them, and re-layouts: 2.28 us -> 1.3 us
    concatenate x0 -> x1, other arithmetic: none -> 0.77 us  [per_device(): named = jnp.concatenate([picks, super_ids], axis=1)]
where the time goes in v4:
time: 46.6 us; the launch traced here: 46.5 us
  Pallas kernels  43.7 us (94%)
  local copies, waits for them, and re-layouts  1.3 us (3%)
  other arithmetic  0.77 us (2%)
  between operations  0.64 us (1%)
    pallas_call x1, Pallas kernels, per_device(): pl.pallas_call(kernel, out_shape=(jax.ShapeDtypeStruct((nb, s // D, H, D)...  43.7 us
    unnamed x2, local copies, waits for them, and re-layouts  1.3 us

profile of v4, /device:TPU:1, one launch (start us, length us, event | category | flops | bytes accessed | tf_op | source)
XLA Modules:
  0.0 46.5 jit_solution(12955600318733158072)
XLA Ops:
  0.6 0.8 %pad_add_fusion.pk_ref = s32[4,80]{1,0:T(4,128)S(1)} fusion(s32[4,16]{1,0:T(4,128)} %param.8, s32[4,64]{1,0:T(4,128)} %param.9), kind=kLoop, calls=%fused_computation | loop fusion | flops 320 | bytes 2560 | tf_op jit(solution)/shard_map/concatenate | solution.py:345
  1.4 43.7 %shard_map.68 = (f32[4,16,8,128]{3,2,1,0:T(8,128)S(1)}, f32[4,512]{1,0:T(4,128)S(1)}) custom-call(bf16[4,128,1024]{2,1,0:T(8,128)(2,1)} %q_ref.1, bf16[256,1024]{1,0:T(8,128)(2,1)} %ck_ref.1, bf16[64,8,1024]{2,1,0:T(8,128)(2,1)} %bitcast.5, s32[4,80]{1,0:T(4,128)S(1)} %pad_add_fusion.pk_ref), custom_call_target="tpu_custom_call" | custom-call | tf_op jit(solution)/shard_map/pallas_call | solution.py:346
  45.2 0.7 %copy.9 = f32[4,8,2048]{2,1,0:T(8,128)} copy(f32[4,8,2048]{2,1,0:T(8,128)S(1)} %bitcast.4) | data formatting | bytes 524288
  45.9 0.6 %copy.10 = f32[4,512]{1,0:T(4,128)} copy(f32[4,512]{1,0:T(4,128)S(1)} %get-tuple-element.9) | data formatting | bytes 16384

commit v5 on v4

--- a/solution.py
+++ b/solution.py
@@ -283,17 +283,18 @@
             fres[g, b:b + 1, :] = jnp.sum(jnp.where(hits(g, b), val, 0.0), axis=0, keepdims=True)
 
     def fine_step(n, carry):
-        m = G - n
-
-        @pl.when(n > 1)
-        def _():
+        m = G - 1 - 2 * n
+
+        @pl.when(n > 0)
+        def _():
+            send_picked(m + 2).start()
             send_picked(m + 1).start()
 
         fine(m)
+        fine(m - 1)
         return carry
 
-    lax.fori_loop(1, G, fine_step, 0)
-    fine(0)
+    lax.fori_loop(0, G // 2, fine_step, 0)
     send_picked(1).start()
     frecv[me] = fres[me]
     irecv[me] = res[me]

time: 46.6 us -> 46 us (0.987)
  Pallas kernels: 43.7 us -> 43.2 us
    pallas_call x1, Pallas kernels: 43.7 us -> 43.2 us  [per_device(): pl.pallas_call(kernel, out_shape=(jax.ShapeDtypeStruct((nb, s // D, H, D)...]
where the time goes in v5:
time: 46 us; the launch traced here: 45.9 us
  Pallas kernels  43.2 us (94%)
  local copies, waits for them, and re-layouts  1.3 us (3%)
  other arithmetic  0.77 us (2%)
  between operations  0.64 us (1%)
    pallas_call x1, Pallas kernels, per_device(): pl.pallas_call(kernel, out_shape=(jax.ShapeDtypeStruct((nb, s // D, H, D)...  43.2 us
    unnamed x2, local copies, waits for them, and re-layouts  1.3 us

profile of v5, /device:TPU:1, one launch (start us, length us, event | category | flops | bytes accessed | tf_op | source)
XLA Modules:
  0.0 45.9 jit_solution(7120001920587313334)
XLA Ops:
  0.6 0.8 %pad_add_fusion.pk_ref = s32[4,80]{1,0:T(4,128)S(1)} fusion(s32[4,16]{1,0:T(4,128)} %param.8, s32[4,64]{1,0:T(4,128)} %param.9), kind=kLoop, calls=%fused_computation | loop fusion | flops 320 | bytes 2560 | tf_op jit(solution)/shard_map/concatenate | solution.py:346
  1.4 43.2 %shard_map.68 = (f32[4,16,8,128]{3,2,1,0:T(8,128)S(1)}, f32[4,512]{1,0:T(4,128)S(1)}) custom-call(bf16[4,128,1024]{2,1,0:T(8,128)(2,1)} %q_ref.1, bf16[256,1024]{1,0:T(8,128)(2,1)} %ck_ref.1, bf16[64,8,1024]{2,1,0:T(8,128)(2,1)} %bitcast.5, s32[4,80]{1,0:T(4,128)S(1)} %pad_add_fusion.pk_ref), custom_call_target="tpu_custom_call" | custom-call | tf_op jit(solution)/shard_map/pallas_call | solution.py:347
  44.6 0.7 %copy.9 = f32[4,8,2048]{2,1,0:T(8,128)} copy(f32[4,8,2048]{2,1,0:T(8,128)S(1)} %bitcast.4) | data formatting | bytes 524288
  45.3 0.6 %copy.10 = f32[4,512]{1,0:T(4,128)} copy(f32[4,512]{1,0:T(4,128)S(1)} %get-tuple-element.9) | data formatting | bytes 16384

commit v6 on v5

--- a/solution.py
+++ b/solution.py
@@ -236,7 +236,7 @@
                 bias[g, b] = jnp.broadcast_to(jnp.where(found > 0.0, 0.0, -1e30), (NSEL * SBLK, T))
             return carry
 
-        lax.fori_loop(0, G, one, 0)
+        lax.fori_loop(0, G, one, 0, unroll=2)
         to_smem.wait()
 
     masks()

time: 46 us -> 46 us (level)
  no operation moved by 1% of the time
where the time goes in v6:
time: 46 us; the launch traced here: 45.9 us
  Pallas kernels  43.2 us (94%)
  local copies, waits for them, and re-layouts  1.3 us (3%)
  other arithmetic  0.77 us (2%)
  between operations  0.64 us (1%)
    pallas_call x1, Pallas kernels, per_device(): pl.pallas_call(kernel, out_shape=(jax.ShapeDtypeStruct((nb, s // D, H, D)...  43.2 us
    unnamed x2, local copies, waits for them, and re-layouts  1.3 us

profile of v6, /device:TPU:1, one launch (start us, length us, event | category | flops | bytes accessed | tf_op | source)
XLA Modules:
  0.0 45.9 jit_solution(5262505264111644487)
XLA Ops:
  0.6 0.8 %pad_add_fusion.pk_ref = s32[4,80]{1,0:T(4,128)S(1)} fusion(s32[4,16]{1,0:T(4,128)} %param.8, s32[4,64]{1,0:T(4,128)} %param.9), kind=kLoop, calls=%fused_computation | loop fusion | flops 320 | bytes 2560 | tf_op jit(solution)/shard_map/concatenate | solution.py:346
  1.4 43.2 %shard_map.68 = (f32[4,16,8,128]{3,2,1,0:T(8,128)S(1)}, f32[4,512]{1,0:T(4,128)S(1)}) custom-call(bf16[4,128,1024]{2,1,0:T(8,128)(2,1)} %q_ref.1, bf16[256,1024]{1,0:T(8,128)(2,1)} %ck_ref.1, bf16[64,8,1024]{2,1,0:T(8,128)(2,1)} %bitcast.5, s32[4,80]{1,0:T(4,128)S(1)} %pad_add_fusion.pk_ref), custom_call_target="tpu_custom_call" | custom-call | tf_op jit(solution)/shard_map/pallas_call | solution.py:347
  44.6 0.7 %copy.9 = f32[4,8,2048]{2,1,0:T(8,128)} copy(f32[4,8,2048]{2,1,0:T(8,128)S(1)} %bitcast.4) | data formatting | bytes 524288
  45.3 0.6 %copy.10 = f32[4,512]{1,0:T(4,128)} copy(f32[4,512]{1,0:T(4,128)S(1)} %get-tuple-element.9) | data formatting | bytes 16384
